TPU v7x, 32 devices: a whole 2x2x4 slice. The times are simulated.
32 devices in a mesh: dp: 8 (over z, y), section: 4 (over x, core).
Axes of the slice: x: 2, y: 2, z: 4, core: 2. Of those that a mesh axis runs over, the one named last changes fastest.
Arguments:
- embedded: bfloat16 [8, 8, 16, 1024], P('dp'), may hold values from -6 to 6
- lengths: int32 [8, 8], P('dp'), may hold values from 1 to 16
- counts: int32 [8], P('dp'), may hold values from 4 to 8
- labels: int32 [8, 8], P('dp'), may hold values from 0 to 4
- value_weight: bfloat16 [4, 1024, 1024], P('section', 'dp'), may hold values from -0.1875 to 0.1875
- output_projection_weight: bfloat16 [4, 1024, 1024], P('section', 'dp'), may hold values from -0.1875 to 0.1875
- adapter: float32 [4, 1024, 2, 128], P('section', 'dp'), may hold values from -0.1875 to 0.1875
- moment1: float32 [4, 1024, 2, 128], P('section', 'dp'), may hold values from -0.06 to 0.06
- moment2: float32 [4, 1024, 2, 128], P('section', 'dp'), may hold values from 1e-05 to 0.001
- gain: float32 [4, 1024], P('section'), may hold values from 0.25 to 1.75
- position_bias: float32 [4, 16, 16, 16], P('section'), as said below
- head: float32 [1024], replicated, may hold values from -0.1875 to 0.1875
Outputs:
- new_moment1: float32 [4, 1024, 2, 128], P('section', 'dp')
- new_moment2: float32 [4, 1024, 2, 128], P('section', 'dp')
- update: float32 [4, 1024, 2, 128], P('section', 'dp')
Inputs may be any that keep to these rules, and one draw needn't show every extreme that they name: `counts`: passages of a query group that take part; those at positions counts and beyond are padding. `lengths`: tokens of a passage that are not padding, the first ones. `position_bias`: real logits.
All inputs are finite; a program needn't handle non-finite values.
Results may differ from a plain program's by a relative error of at most 0.018.
Values may be sent and summed in bfloat16 or wider, within the bound.
No kernel may reach another device: no remote copies, remote signals or barrier semaphores. Data moves between devices by JAX's collectives and lax.ppermute only.
A program may use at most 64 MiB of HBM per device.

v0:
```python
import jax
import jax.numpy as jnp
from jax import lax
from jax.sharding import PartitionSpec as P


def shifted(array, axis, by):
    size = lax.axis_size(axis)
    pairs = [(i, i + by) for i in range(size) if 0 <= i + by < size]
    return lax.ppermute(array, axis, pairs)


def probabilities(bias, lens):
    seqlen = bias.shape[-1]
    valid = jnp.arange(seqlen, dtype=jnp.int32)[None, :] < lens[:, None]
    logits = jnp.where(valid[:, None, None, :], bias[None], -1e30)
    top = jnp.max(logits, axis=-1, keepdims=True)
    expo = jnp.exp(logits - top)
    return (expo / jnp.sum(expo, axis=-1, keepdims=True)).astype(jnp.bfloat16)


def section_forward(x, lens, frozen, g, bias):
    value_matrix, w_out, adapt = frozen
    passages = lens.shape[0]
    heads = bias.shape[0]
    input_flat = x.astype(jnp.float32)
    inverse_scale = jnp.sqrt(jnp.mean(input_flat * input_flat, axis=-1, keepdims=True) + 1e-06)
    normed = (input_flat / inverse_scale * g).astype(jnp.bfloat16)
    value = jnp.dot(normed, value_matrix, preferred_element_type=jnp.float32).astype(jnp.bfloat16)
    probs = probabilities(bias, lens)
    value4 = value.reshape(passages, -1, heads, value.shape[1] // heads)
    attn = jnp.einsum("phij,pjhs->pihs", probs, value4, preferred_element_type=jnp.float32)
    attn = attn.astype(jnp.bfloat16).reshape(x.shape[0], -1)
    outer = jnp.einsum("rk,dk->rd", attn, w_out, preferred_element_type=jnp.float32)
    latent = jnp.dot(normed, adapt[:, 0], preferred_element_type=jnp.float32).astype(jnp.bfloat16)
    adapted = jnp.einsum("rk,dk->rd", latent, adapt[:, 1], preferred_element_type=jnp.float32)
    return ((input_flat + outer + adapted).astype(jnp.bfloat16), normed, latent, probs)


def spare_forward(x, lens, frozen, g, bias):
    rank_width = frozen[2].shape[2]
    latent = jnp.zeros((x.shape[0], rank_width), jnp.bfloat16)
    probs = jnp.zeros((lens.shape[0],) + bias.shape, jnp.bfloat16)
    return (x, x, latent, probs)


def section_backward(grad_out, x, probs, frozen, g):
    value_matrix, w_out, adapt = frozen
    passages, heads = (probs.shape[0], probs.shape[1])
    output_gradient_flat = grad_out.astype(jnp.float32)
    dattn = jnp.dot(grad_out, w_out, preferred_element_type=jnp.float32).astype(jnp.bfloat16)
    d4 = dattn.reshape(passages, -1, heads, dattn.shape[1] // heads)
    dvalue = jnp.einsum("phij,pihs->pjhs", probs, d4, preferred_element_type=jnp.float32)
    dvalue = dvalue.astype(jnp.bfloat16).reshape(x.shape[0], -1)
    dlatent = jnp.dot(grad_out, adapt[:, 1], preferred_element_type=jnp.float32).astype(
        jnp.bfloat16
    )
    da = jnp.einsum("rk,dk->rd", dvalue, value_matrix, preferred_element_type=jnp.float32)
    da = da + jnp.einsum("rk,dk->rd", dlatent, adapt[:, 0], preferred_element_type=jnp.float32)
    input_flat = x.astype(jnp.float32)
    inverse_scale = jnp.sqrt(jnp.mean(input_flat * input_flat, axis=-1, keepdims=True) + 1e-06)
    input_standardized = input_flat / inverse_scale
    norm_gradient = da * g
    input_gradient = (
        output_gradient_flat
        + (
            norm_gradient
            - input_standardized
            * jnp.mean(norm_gradient * input_standardized, axis=-1, keepdims=True)
        )
        / inverse_scale
    )
    return (input_gradient.astype(jnp.bfloat16), dlatent)


def spare_backward(grad_out, x, probs, frozen, g):
    rank_width = frozen[2].shape[2]
    return (grad_out, jnp.zeros((x.shape[0], rank_width), jnp.bfloat16))


def adapter_term(normed, latent, grad_out, dlatent):
    term_down = jnp.einsum("rd,rk->dk", normed, dlatent, preferred_element_type=jnp.float32)
    term_up = jnp.einsum("rd,rk->dk", grad_out, latent, preferred_element_type=jnp.float32)
    return jnp.stack([term_down, term_up], axis=1)


def no_term(normed, latent, grad_out, dlatent):
    return jnp.zeros((normed.shape[1], 2, latent.shape[1]), jnp.float32)


def group_loss(scores, lab, count):
    idx = jnp.arange(lab.shape[0], dtype=jnp.int32)
    valid = idx < count
    left = lab[:, None]
    right = lab[None, :]
    before = ((right > left) | (right == left) & (idx[None, :] < idx[:, None])) & valid[None, :]
    rank = jnp.sum(before.astype(jnp.int32), axis=1)
    gains = jnp.exp2(lab.astype(jnp.float32)) - 1.0
    disc = 1.0 / jnp.log2(2.0 + rank.astype(jnp.float32))
    pair = (left > right) & valid[:, None] & valid[None, :]
    weights = jnp.where(
        pair, jnp.abs(gains[:, None] - gains[None, :]) * jnp.abs(disc[:, None] - disc[None, :]), 0.0
    )
    ideal = jnp.sum(jnp.where(valid, gains * disc, 0.0))
    margin = scores[:, None] - scores[None, :]
    return jnp.sum(weights * jax.nn.softplus(-margin)) / jnp.maximum(ideal, 1.0)


def loss_cotangent(final, lens, count, lab, head):
    tokens = final.shape[1]
    mask = jnp.arange(tokens, dtype=jnp.int32)[None, :] < lens[:, None]
    pooled = jnp.einsum(
        "pt,ptd->pd", mask.astype(jnp.bfloat16), final, preferred_element_type=jnp.float32
    )
    denom = lens.astype(jnp.float32)
    scores = jnp.dot(pooled / denom[:, None], head, precision=lax.Precision.HIGHEST)
    dscore = jax.grad(group_loss)(scores, lab, count)
    cot = (
        dscore[:, None, None]
        * head[None, None, :]
        * mask.astype(jnp.float32)[:, :, None]
        / denom[:, None, None]
    )
    return cot.astype(jnp.bfloat16)


def pick(buffer, position):
    return lax.dynamic_index_in_dim(buffer, position, 0, False)


def store(buffer, value, position, active):
    kept = jnp.where(active, value, pick(buffer, position))
    return lax.dynamic_update_index_in_dim(buffer, kept, position, 0)


def shards(
    embedded,
    lengths,
    counts,
    labels,
    value_weight,
    output_projection_weight,
    adapter,
    moment1,
    moment2,
    gain,
    position_bias,
    head,
):
    sections = lax.axis_size("section")
    section_index = lax.axis_index("section")
    groups, passages, seqlen, width = embedded.shape
    total_rows = passages * seqlen
    shard = (value_weight[0], output_projection_weight[0], adapter[0].astype(jnp.bfloat16))
    frozen = (
        lax.all_gather(shard[0], "dp", axis=0, tiled=True),
        lax.all_gather(shard[1], "dp", axis=0, tiled=True),
        lax.all_gather(shard[2], "dp", axis=0, tiled=True),
    )
    g_row = gain[0]
    bias = position_bias[0]
    heads = bias.shape[0]
    rank_width = adapter.shape[3]
    flat = embedded.reshape(groups, total_rows, width)
    keep_x = jnp.zeros((groups, total_rows, width), jnp.bfloat16)
    keep_n = jnp.zeros((groups, total_rows, width), jnp.bfloat16)
    keep_z = jnp.zeros((groups, total_rows, rank_width), jnp.bfloat16)
    keep_p = jnp.zeros((groups, passages, heads, seqlen, seqlen), jnp.bfloat16)
    keep_y = jnp.zeros((groups, total_rows, width), jnp.bfloat16)
    incoming = jnp.zeros((total_rows, width), jnp.bfloat16)
    ticks = groups + sections - 1
    for tick in range(ticks):
        micro = tick - section_index
        active = (micro >= 0) & (micro < groups)
        position = jnp.clip(micro, 0, groups - 1)
        source = jnp.where(section_index == 0, pick(flat, position), incoming)
        lens = pick(lengths, position)
        out_rows, normed, latent, probs = lax.cond(
            active, section_forward, spare_forward, source, lens, frozen, g_row, bias
        )
        keep_x = store(keep_x, source, position, active)
        keep_n = store(keep_n, normed, position, active)
        keep_z = store(keep_z, latent, position, active)
        keep_p = store(keep_p, probs, position, active)
        keep_y = store(keep_y, out_rows, position, active)
        incoming = shifted(out_rows, "section", 1)
    finals = keep_y.reshape(groups, passages, seqlen, width)
    cotangent = jax.vmap(loss_cotangent, in_axes=(0, 0, 0, 0, None))(
        finals, lengths, counts, labels, head
    )
    cotangent = cotangent.reshape(groups, total_rows, width)
    total = jnp.zeros((width, 2, rank_width), jnp.float32)
    first_dy = jnp.zeros((total_rows, width), jnp.bfloat16)
    first_dz = jnp.zeros((total_rows, rank_width), jnp.bfloat16)
    returning = jnp.zeros((total_rows, width), jnp.bfloat16)
    for tick in range(ticks):
        micro = groups - 1 - (tick - (sections - 1 - section_index))
        active = (micro >= 0) & (micro < groups)
        position = jnp.clip(micro, 0, groups - 1)
        upstream = jnp.where(section_index == sections - 1, pick(cotangent, position), returning)
        normed = pick(keep_n, position)
        latent = pick(keep_z, position)
        input_gradient, dlatent = lax.cond(
            active,
            section_backward,
            spare_backward,
            upstream,
            pick(keep_x, position),
            pick(keep_p, position),
            frozen,
            g_row,
        )
        counted = active & (micro != 0)
        is_first = active & (micro == 0)
        first_dy = jnp.where(is_first, upstream, first_dy)
        first_dz = jnp.where(is_first, dlatent, first_dz)
        total = total + lax.cond(counted, adapter_term, no_term, normed, latent, upstream, dlatent)
        returning = shifted(input_gradient, "section", -1)
    first_normed = keep_n[0]
    first_latent = keep_z[0]
    extra = adapter_term(first_normed, first_latent, first_dy, first_dz)
    grad = lax.psum_scatter(total + extra, "dp", scatter_dimension=0, tiled=True)
    new_moment1 = 0.9 * moment1[0] + 0.1 * grad
    new_moment2 = 0.999 * moment2[0] + 0.001 * grad * grad
    update = new_moment1 / (1.0 - 0.9**10) / (jnp.sqrt(new_moment2 / (1.0 - 0.999**10)) + 1e-08)
    return (new_moment1[None], new_moment2[None], update[None])


def solution(mesh):
    in_specs = (
        P("dp", None, None, None),
        P("dp", None),
        P("dp"),
        P("dp", None),
        P("section", "dp", None),
        P("section", "dp", None),
        P("section", "dp", None, None),
        P("section", "dp", None, None),
        P("section", "dp", None, None),
        P("section", None),
        P("section", None, None, None),
        P(),
    )
    out_specs = (
        P("section", "dp", None, None),
        P("section", "dp", None, None),
        P("section", "dp", None, None),
    )
    return jax.shard_map(shards, mesh=mesh, in_specs=in_specs, out_specs=out_specs, check_vma=False)
```

profile of v0, /device:TPU:0, one launch (start us, length us, event | category | flops | bytes accessed | tf_op | source)
XLA Modules:
  0.0 336.4 jit_solution(3929584598555748127)
XLA Ops:
  9.6 34.2 %all-gather.2 = bf16[1,1024,2,128]{3,1,2,0:T(8,128)(2,1)S(1)} all-gather(bf16[1,128,2,128]{3,1,2,0:T(8,128)(2,1)S(1)} %copy.122), channel_id=4, replica_groups=mesh['dp'=8,'section'=4] {'dp'}, dimensions={1}, use_global_device_ids=true | all-gather | bytes 589824 | tf_op jit(solution)/shard_map/all_gather | solution.py:158
  44.8 19.0 %all-gather.6.cloned.1.call-done = bf16[1,1024,1024]{2,1,0:T(8,128)(2,1)} async-done(((bf16[1,128,1024]{2,1,0:T(8,128)(2,1)}), bf16[1,1024,1024]{2,1,0:T(8,128)(2,1)}) %all-gather.6.cloned.1.call-update) | async-done | bytes 2097168 | tf_op jit(solution)/shard_map/all_gather | solution.py:156
  63.7 50.3 %all-gather.8.cloned.1.call-done = bf16[1,1024,1024]{2,1,0:T(8,128)(2,1)} async-done(((bf16[1,128,1024]{2,1,0:T(8,128)(2,1)}), bf16[1,1024,1024]{2,1,0:T(8,128)(2,1)}) %all-gather.8.cloned.1.call-update) | async-done | bytes 2097168 | tf_op jit(solution)/shard_map/all_gather | solution.py:157
  114.0 16.1 %conditional.12 = (bf16[128,1024]{1,0:T(8,128)(2,1)S(1)}, bf16[128,1024]{1,0:T(8,128)(2,1)}, bf16[128,128]{1,0:T(8,128)(2,1)}, bf16[8,16,16,16]{2,3,1,0:T(8,128)(2,1)S(1)}) conditional(s32[]{:T(128)} %convert_element_type.263, bf16[128,1024]{1,0:T(8,128)(2,1)S(1)} %bitcast_select_fusion.3, (bf16[128,1024]{1,0:T(8,128)(2,1)S(1)}, f32[1,1024]{1,0:T(1,128)}, ...), branch_computations={%region_0.1_spmd, %region_1.5_spmd} | conditional | flops 610091264 | bytes 27646356 | solution.py:178
  114.9 1.6 fusion.150
  116.5 1.1 divide_convert_fusion
  118.6 1.4 convolution_convert_fusion.1
  120.0 1.1 reshape.975
  121.2 1.6 fusion.7
  123.7 1.4 reshape.976
  126.0 1.8 convolution_convert_fusion.2
  128.8 1.3 copy.82
  130.1 1.3 collective-permute-start
  131.4 1.1 collective-permute-done
  132.6 2.3 conditional.13
  134.9 17.3 %collective-permute-start.1 = (bf16[128,1024]{1,0:T(8,128)(2,1)}, bf16[128,1024]{1,0:T(8,128)(2,1)S(1)}, u32[]{:S(2)}, u32[]{:S(2)}) collective-permute-start(bf16[128,1024]{1,0:T(8,128)(2,1)} %get-tuple-element.249), channel_id=1, source_target_pairs={{0,1},{1,2},{2,3},{4,5},{5,6},{6,7},{8,9},{9,10},{10,11},{12,13},{... | collective-permute-start | bytes 786440 | tf_op jit(solution)/shard_map/ppermute | solution.py:10
  154.6 2.9 conditional.14
  157.5 4.1 %collective-permute-start.2 = (bf16[128,1024]{1,0:T(8,128)(2,1)}, bf16[128,1024]{1,0:T(8,128)(2,1)S(1)}, u32[]{:S(2)}, u32[]{:S(2)}) collective-permute-start(bf16[128,1024]{1,0:T(8,128)(2,1)} %get-tuple-element.250), channel_id=1, source_target_pairs={{0,1},{1,2},{2,3},{4,5},{5,6},{6,7},{8,9},{9,10},{10,11},{12,13},{... | collective-permute-start | bytes 786440 | tf_op jit(solution)/shard_map/ppermute | solution.py:10
  164.5 2.2 conditional.15
  167.4 1.2 select_select_fusion.2
  171.0 1.3 collective-permute-start.3
  172.3 21.2 %collective-permute-done.3 = bf16[128,1024]{1,0:T(8,128)(2,1)} collective-permute-done((bf16[128,1024]{1,0:T(8,128)(2,1)S(1)}, bf16[128,1024]{1,0:T(8,128)(2,1)}, u32[]{:S(2)}, u32[]{:S(2)}) %collective-permute-start.3) | collective-permute-done | bytes 262176 | tf_op jit(solution)/shard_map/ppermute | solution.py:10
  193.6 1.1 broadcast_select_fusion.2
  194.7 1.3 conditional.18
  196.0 1.3 collective-permute-start.4
  197.4 7.3 %collective-permute-done.4 = bf16[128,1024]{1,0:T(8,128)(2,1)} collective-permute-done((bf16[128,1024]{1,0:T(8,128)(2,1)}, bf16[128,1024]{1,0:T(8,128)(2,1)}, u32[]{:S(2)}, u32[]{:S(2)}) %collective-permute-start.4) | collective-permute-done | bytes 262176 | tf_op jit(solution)/shard_map/ppermute | solution.py:10
  204.7 1.1 broadcast_select_fusion.1
  205.8 1.3 conditional.20
  207.1 1.3 collective-permute-start.5
  212.4 42.4 %collective-permute-done.5 = bf16[128,1024]{1,0:T(8,128)(2,1)} collective-permute-done((bf16[128,1024]{1,0:T(8,128)(2,1)}, bf16[128,1024]{1,0:T(8,128)(2,1)}, u32[]{:S(2)}, u32[]{:S(2)}) %collective-permute-start.5) | collective-permute-done | bytes 262176 | tf_op jit(solution)/shard_map/ppermute | solution.py:10
  256.9 2.8 maximum_add_fusion
  259.7 66.9 %reduce-scatter.2.cloned.1.call-done = f32[128,2,128]{2,0,1:T(8,128)} async-done(((f32[1024,2,128]{2,0,1:T(8,128)}), f32[128,2,128]{2,0,1:T(8,128)}) %reduce-scatter.2.cloned.1.call-update) | async-done | bytes 131088 | tf_op jit(solution)/shard_map/reduce_scatter | solution.py:222
  (108 shorter events, 37.4 us)
Async XLA Ops:
  7.2 56.6 %all-gather.6.cloned.1.call-start = ((), (), s32[]{:S(2)}) async-start(), calls=%async_computation.2 | async-start | bytes 2359296 | tf_op jit(solution)/shard_map/all_gather | solution.py:156
  7.9 106.1 %all-gather.8.cloned.1.call-start = ((), (), s32[]{:S(2)}) async-start(), calls=%async_computation.3 | async-start | bytes 2359296 | tf_op jit(solution)/shard_map/all_gather | solution.py:157
  8.6 317.9 %reduce-scatter.2.cloned.1.call-start = ((), (), s32[]{:S(2)}) async-start(), calls=%async_computation.1 | async-start | bytes 1179648 | tf_op jit(solution)/shard_map/reduce_scatter | solution.py:222
  114.0 18.6 %copy-start.18 = (bf16[1,8,16,1024]{3,2,1,0:T(8,128)(2,1)S(1)}, bf16[1,8,16,1024]{3,2,1,0:T(8,128)(2,1)}, u32[]{:S(2)}) copy-start(bf16[1,8,16,1024]{3,2,1,0:T(8,128)(2,1)} %param.36) | copy-start | bytes 786436
  114.0 3.8 %copy-start.24 = (f32[1,1024]{1,0:T(1,128)S(1)}, f32[1,1024]{1,0:T(1,128)}, u32[]{:S(2)}) copy-start(f32[1,1024]{1,0:T(1,128)} %get-tuple-element.157) | copy-start | bytes 12292 | tf_op jit(solution)/shard_map/cond
  114.0 4.6 %copy-start.1 = (bf16[1024,1024]{1,0:T(8,128)(2,1)S(1)}, bf16[1024,1024]{1,0:T(8,128)(2,1)}, u32[]{:S(2)}) copy-start(bf16[1024,1024]{1,0:T(8,128)(2,1)} %get-tuple-element.158) | copy-start | bytes 6291460 | tf_op jit(solution)/shard_map/cond
  120.0 5.1 %copy-start.6 = (bf16[1024,1024]{1,0:T(8,128)(2,1)S(1)}, bf16[1024,1024]{1,0:T(8,128)(2,1)}, u32[]{:S(2)}) copy-start(bf16[1024,1024]{1,0:T(8,128)(2,1)} %get-tuple-element.161) | copy-start | bytes 6291460 | tf_op jit(solution)/shard_map/cond
  130.1 2.5 copy-start.19
  130.1 2.5 copy-start.12
  130.1 2.4 collective-permute-start
  132.6 20.9 %copy-start.30 = (s32[1,8]{1,0:T(1,128)S(1)}, s32[1,8]{1,0:T(1,128)}, u32[]{:S(2)}) copy-start(s32[1,8]{1,0:T(1,128)} %param.37) | copy-start | bytes 100
  134.9 19.7 %copy-start.17 = (bf16[128,1024]{1,0:T(8,128)(2,1)}, bf16[128,1024]{1,0:T(8,128)(2,1)S(1)}, u32[]{:S(2)}) copy-start(bf16[128,1024]{1,0:T(8,128)(2,1)S(1)} %get-tuple-element.253) | copy-start | bytes 786436
  134.9 18.7 %collective-permute-start.1 = (bf16[128,1024]{1,0:T(8,128)(2,1)}, bf16[128,1024]{1,0:T(8,128)(2,1)S(1)}, u32[]{:S(2)}, u32[]{:S(2)}) collective-permute-start(bf16[128,1024]{1,0:T(8,128)(2,1)} %get-tuple-element.249), channel_id=1, source_target_pairs={{0,1},{1,2},{2,3},{4,5},{5,6},{6,7},{8,9},{9,10},{10,11},{12,13},{... | collective-permute-start | bytes 786440 | tf_op jit(solution)/shard_map/ppermute | solution.py:10
  154.6 7.4 %copy-start.28 = (s32[1,8]{1,0:T(1,128)S(1)}, s32[1,8]{1,0:T(1,128)}, u32[]{:S(2)}) copy-start(s32[1,8]{1,0:T(1,128)} %param.39) | copy-start | bytes 100
  157.5 5.9 %collective-permute-start.2 = (bf16[128,1024]{1,0:T(8,128)(2,1)}, bf16[128,1024]{1,0:T(8,128)(2,1)S(1)}, u32[]{:S(2)}, u32[]{:S(2)}) collective-permute-start(bf16[128,1024]{1,0:T(8,128)(2,1)} %get-tuple-element.250), channel_id=1, source_target_pairs={{0,1},{1,2},{2,3},{4,5},{5,6},{6,7},{8,9},{9,10},{10,11},{12,13},{... | collective-permute-start | bytes 786440 | tf_op jit(solution)/shard_map/ppermute | solution.py:10
  164.4 30.3 %copy-start.10 = (bf16[128,1024]{1,0:T(8,128)(2,1)}, bf16[128,1024]{1,0:T(8,128)(2,1)S(1)}, u32[]{:S(2)}) copy-start(bf16[128,1024]{1,0:T(8,128)(2,1)S(1)} %get-tuple-element.285) | copy-start | bytes 786436
  164.5 4.3 %copy-start.29 = (f32[1024]{0:T(1024)S(1)}, f32[1024]{0:T(1024)}, u32[]{:S(2)}) copy-start(f32[1024]{0:T(1024)} %param.47) | copy-start | bytes 12292
  166.7 0.7 copy-start.13
  167.4 2.1 copy-start.20
  167.4 3.0 copy-start
  167.4 3.0 copy-start.5
  167.4 3.0 copy-start.23
  171.0 22.5 %collective-permute-start.3 = (bf16[128,1024]{1,0:T(8,128)(2,1)S(1)}, bf16[128,1024]{1,0:T(8,128)(2,1)}, u32[]{:S(2)}, u32[]{:S(2)}) collective-permute-start(bf16[128,1024]{1,0:T(8,128)(2,1)S(1)} %get-tuple-element.265), channel_id=1, source_target_pairs={{1,0},{2,1},{3,2},{5,4},{6,5},{7,6},{9,8},{10,9},{11,10},{13,12},{... | collective-permute-start | bytes 786440 | tf_op jit(solution)/shard_map/ppermute | solution.py:10
  196.0 8.6 %collective-permute-start.4 = (bf16[128,1024]{1,0:T(8,128)(2,1)}, bf16[128,1024]{1,0:T(8,128)(2,1)}, u32[]{:S(2)}, u32[]{:S(2)}) collective-permute-start(bf16[128,1024]{1,0:T(8,128)(2,1)} %get-tuple-element.267), channel_id=1, source_target_pairs={{1,0},{2,1},{3,2},{5,4},{6,5},{7,6},{9,8},{10,9},{11,10},{13,12},{... | collective-permute-start | bytes 786440 | tf_op jit(solution)/shard_map/ppermute | solution.py:10
  207.1 47.7 %collective-permute-start.5 = (bf16[128,1024]{1,0:T(8,128)(2,1)}, bf16[128,1024]{1,0:T(8,128)(2,1)}, u32[]{:S(2)}, u32[]{:S(2)}) collective-permute-start(bf16[128,1024]{1,0:T(8,128)(2,1)} %get-tuple-element.269), channel_id=1, source_target_pairs={{1,0},{2,1},{3,2},{5,4},{6,5},{7,6},{9,8},{10,9},{11,10},{13,12},{... | collective-permute-start | bytes 786440 | tf_op jit(solution)/shard_map/ppermute | solution.py:10
  256.9 69.7 %copy-start.21 = (f32[1,128,2,128]{3,2,1,0:T(2,128)S(1)}, f32[1,128,2,128]{3,2,1,0:T(2,128)}, u32[]{:S(2)}) copy-start(f32[1,128,2,128]{3,2,1,0:T(2,128)} %param.43) | copy-start | bytes 393220
  256.9 69.7 %copy-start.22 = (f32[1,128,2,128]{3,2,1,0:T(2,128)S(1)}, f32[1,128,2,128]{3,2,1,0:T(2,128)}, u32[]{:S(2)}) copy-start(f32[1,128,2,128]{3,2,1,0:T(2,128)} %param.44) | copy-start | bytes 393220
Sparse Core Ops, SparseCore 0:
  10.1 53.5 all-gather.5
  65.9 48.0 all-gather.7
  259.8 66.6 reduce-scatter.1
where the time goes:
time: 338 us; the launch traced here: 336 us
  waiting for transfers between devices  210 us (62%)
  blocking collectives  34.2 us (10%)
  starting transfers between devices  26.7 us (8%)
  local copies, waits for them, and re-layouts  21.8 us (6%)
  other arithmetic  20.7 us (6%)
  between operations  15.5 us (5%)
  matrix products  7.78 us (2%)
    ppermute x6, waiting for transfers between devices, shifted(): return lax.ppermute(array, axis, pairs)  72 us
    reduce_scatter x1, waiting for transfers between devices, shards(): lax.psum_scatter(total + extra, 'dp', scatter_dimension=0, tiled=True)  66.9 us
    all_gather x1, waiting for transfers between devices, shards(): lax.all_gather(shard[1], 'dp', axis=0, tiled=True)  50.3 us
    all_gather x1, blocking collectives, shards(): lax.all_gather(shard[2], 'dp', axis=0, tiled=True)  34.2 us
    ppermute x6, starting transfers between devices, shifted(): return lax.ppermute(array, axis, pairs)  26.6 us
    all_gather x1, waiting for transfers between devices, shards(): lax.all_gather(shard[0], 'dp', axis=0, tiled=True)  19 us
    another operation x13, local copies, waits for them, and re-layouts  8.56 us
  transfers between devices with their start and end apart: 9, of which 7 were waited for; matrix products, arithmetic and copies ran while one was open for 2% of the time, Pallas kernels for 0%

commit v1 on v0

v1 whole, which is shorter than its diff:
```python
import functools

import jax
import jax.numpy as jnp
from jax import lax
from jax.experimental import pallas as pl
from jax.experimental.pallas import tpu as pltpu
from jax.sharding import PartitionSpec as P


F32 = jnp.float32
BF16 = jnp.bfloat16
LANES = 128
NN = (((1,), (0,)), ((), ()))
NT = (((1,), (1,)), ((), ()))
TN = (((0,), (0,)), ((), ()))
VMEM = pl.BlockSpec(memory_space=pltpu.VMEM)
SMEM = pl.BlockSpec(memory_space=pltpu.SMEM)
ANY = pl.BlockSpec(memory_space=pl.ANY)


def limit(mib):
    return pltpu.CompilerParams(vmem_limit_bytes=mib * 1024 * 1024)


def dot(a, b, dims=NN):
    return lax.dot_general(a, b, dims, preferred_element_type=F32)


def step_of(width):
    return 256 if width % 256 == 0 else width


def dp_index():
    return lax.axis_index("dp")


def pack_kernel(out_ref, adapter_ref, joined_ref):
    wide = out_ref.shape[1]
    rank = adapter_ref.shape[2]
    joined_ref[:, :wide] = out_ref[...]
    for k in range(adapter_ref.shape[1]):
        at = wide + k * rank
        joined_ref[:, at : at + rank] = adapter_ref[:, k, :].astype(BF16)


def assemble_kernel(sources, size, *refs):
    outer, inner = split(size)
    arrays = refs[: len(sources)]
    whole, sems = refs[-2:]
    index = dp_index()
    copies = []
    for at, (far, near) in enumerate(sources):
        rows = arrays[at].shape[0]
        z = (index // inner + far + outer) % outer
        y = (index + near) % inner
        begin = pl.multiple_of((z * inner + y) * rows, rows)
        copies.append(pltpu.make_async_copy(arrays[at], whole.at[pl.ds(begin, rows)], sems.at[at]))
    for copy in copies:
        copy.start()
    for copy in copies:
        copy.wait()


def assemble(arrays, sources, size, earlier=None):
    count = len(arrays)
    rows, columns = arrays[0].shape
    more = [] if earlier is None else [earlier]
    return pl.pallas_call(
        functools.partial(assemble_kernel, sources, size),
        out_shape=jax.ShapeDtypeStruct((rows * size, columns), arrays[0].dtype),
        in_specs=[VMEM] * (count + len(more)),
        out_specs=VMEM,
        scratch_shapes=[pltpu.SemaphoreType.DMA((count,))],
        input_output_aliases={count: 0} if more else {},
        compiler_params=limit(8),
        name="assemble",
    )(*arrays, *more)


def transposed(row, eye):
    return jnp.sum(jnp.where(eye, row, 0.0), axis=1, keepdims=True)


def pair_kernel(lens_ref, counts_ref, labels_ref, lengths_ref, pool_ref, poolt_ref, pair_ref, pairt_ref, lenc_ref, lenr_ref):
    groups, count, rows = pool_ref.shape
    seqlen = rows // count
    across = lax.broadcasted_iota(jnp.int32, (count, count), 1)
    along = lax.broadcasted_iota(jnp.int32, (count, count), 0)
    eye = across == along
    for g in range(groups):
        valid_row = across < counts_ref[g]
        valid_col = along < counts_ref[g]
        row = jnp.broadcast_to(labels_ref[g : g + 1, :].astype(F32), (count, count))
        col = jnp.broadcast_to(transposed(row, eye), (count, count))
        ahead = ((col > row) | (col == row) & (along < across)) & valid_col
        disc_row = 1.0 / jnp.log2(2.0 + jnp.sum(ahead.astype(F32), axis=0, keepdims=True))
        ahead = ((row > col) | (row == col) & (across < along)) & valid_row
        disc_col = 1.0 / jnp.log2(2.0 + jnp.sum(ahead.astype(F32), axis=1, keepdims=True))
        gain_row = jnp.exp2(row) - 1.0
        gain_col = jnp.exp2(col) - 1.0
        once = jnp.where(valid_row & (along == 0), gain_row * disc_row, 0.0)
        ideal = jnp.maximum(jnp.sum(jnp.sum(once, axis=1, keepdims=True), axis=0, keepdims=True), 1.0)
        gap = jnp.abs(gain_row - gain_col) * jnp.abs(disc_row - disc_col) / ideal
        valid = valid_row & valid_col
        pair_ref[g] = jnp.where(valid & (col > row), gap, 0.0)
        pairt_ref[g] = jnp.where(valid & (row > col), gap, 0.0)
        lens = lengths_ref[g : g + 1, :].astype(F32)
        lenr_ref[g] = lens
        lenc_ref[g] = transposed(jnp.broadcast_to(lens, (count, count)), eye)
        lane = lax.broadcasted_iota(jnp.int32, (count, rows), 1)
        passage = lax.broadcasted_iota(jnp.int32, (count, rows), 0)
        held = lane % seqlen < lenc_ref[g].astype(jnp.int32)
        pool_ref[g] = ((lane // seqlen == passage) & held).astype(F32).astype(BF16)
        place = lax.broadcasted_iota(jnp.int32, (rows, count), 0)
        passage = lax.broadcasted_iota(jnp.int32, (rows, count), 1)
        held = place % seqlen < lengths_ref[g : g + 1, :]
        poolt_ref[g] = ((place // seqlen == passage) & held).astype(F32)


def prob_kernel(lens_ref, bias_ref, probs_ref, probst_ref):
    heads, seqlen, _ = bias_ref.shape
    groups, _, rows, _ = probs_ref.shape
    passages = rows // seqlen
    spread = lax.broadcasted_iota(jnp.int32, (seqlen, rows), 1) % seqlen
    spread = (spread == lax.broadcasted_iota(jnp.int32, (seqlen, rows), 0)).astype(F32)
    tiled = lax.dot_general(
        bias_ref[...].reshape(heads * seqlen, seqlen),
        spread,
        NN,
        precision=lax.Precision.HIGHEST,
        preferred_element_type=F32,
    )
    lane = lax.broadcasted_iota(jnp.int32, (rows, rows), 1)
    same = lane // seqlen == lax.broadcasted_iota(jnp.int32, (rows, rows), 0) // seqlen
    for g in range(groups):
        held = [jnp.full((seqlen, rows), lens_ref[g, p], jnp.int32) for p in range(passages)]
        mask = same & (lane % seqlen < jnp.concatenate(held, axis=0))
        for h in range(heads):
            block = tiled[h * seqlen : (h + 1) * seqlen]
            logits = jnp.where(mask, jnp.concatenate([block] * passages, axis=0), -1e30)
            expo = jnp.exp(logits - jnp.max(logits, axis=-1, keepdims=True))
            prob = expo / jnp.sum(expo, axis=-1, keepdims=True)
            probs_ref[g, h] = prob.astype(BF16)
            probst_ref[g, h] = prob.T.astype(BF16)


def normalize(x_ref):
    x = x_ref[...].astype(F32)
    r = jnp.sqrt(jnp.mean(x * x, axis=-1, keepdims=True) + 1e-06)
    return x, r


def mix_heads(prob_ref, src_ref, dst_ref, groups, head_width):
    rows = prob_ref.shape[2]
    width = src_ref.shape[1]
    per = max(1, LANES // head_width)
    span = per * head_width
    lane = lax.broadcasted_iota(jnp.int32, (rows, span), 1) // head_width
    for g in range(groups):
        at = pl.ds(g * rows, rows)
        for b in range(width // span):
            cols = pl.ds(b * span, span)
            block = src_ref[at, cols]
            if per == 1:
                mixed = dot(prob_ref[g, b], block)
            else:
                zero = jnp.zeros_like(block)
                stack = jnp.concatenate([jnp.where(lane == i, block, zero) for i in range(per)], axis=0)
                probs = jnp.concatenate([prob_ref[g, b * per + i] for i in range(per)], axis=1)
                mixed = dot(probs, stack)
            dst_ref[at, cols] = mixed.astype(BF16)


def forward_body(x_ref, gain_ref, prob_ref, y_ref, norm_ref, z_ref, wv, wb, value, attn, cfg):
    groups, head_width, width, hd, rank = cfg
    x, r = normalize(x_ref)
    norm_ref[...] = (x / r * gain_ref[...]).astype(BF16)
    step = step_of(hd)
    for c in range(0, hd, step):
        value[:, c : c + step] = dot(norm_ref[...], wv[:, c : c + step]).astype(BF16)
    mix_heads(prob_ref, value, attn, groups, head_width)
    z = dot(norm_ref[...], wb[:, hd : hd + rank]).astype(BF16)
    z_ref[...] = z
    step = step_of(width)
    for c in range(0, width, step):
        out = dot(attn[...], wb[c : c + step, :hd], NT)
        adapted = dot(z, wb[c : c + step, hd + rank :], NT)
        y_ref[:, c : c + step] = (x_ref[:, c : c + step].astype(F32) + out + adapted).astype(BF16)


def backward_body(dy_ref, x_ref, gain_ref, probt_ref, dx_ref, dz_ref, wv, wb, value, attn, cfg):
    groups, head_width, width, hd, rank = cfg
    step = step_of(hd)
    for c in range(0, hd, step):
        value[:, c : c + step] = dot(dy_ref[...], wb[:, c : c + step]).astype(BF16)
    dz_ref[...] = dot(dy_ref[...], wb[:, hd + rank :]).astype(BF16)
    mix_heads(probt_ref, value, attn, groups, head_width)
    step = step_of(width)
    x, r = normalize(x_ref)
    xhat = x / r
    parts = []
    total = jnp.zeros((x.shape[0], 1), F32)
    for c in range(0, width, step):
        da = dot(attn[...], wv[c : c + step, :], NT)
        da = da + dot(dz_ref[...], wb[c : c + step, hd : hd + rank], NT)
        dn = da * gain_ref[:, c : c + step]
        parts.append(dn)
        total = total + jnp.sum(dn * xhat[:, c : c + step], axis=-1, keepdims=True)
    mean = total / width
    for at, c in enumerate(range(0, width, step)):
        dx = (parts[at] - xhat[:, c : c + step] * mean) / r
        dx_ref[:, c : c + step] = (dy_ref[:, c : c + step].astype(F32) + dx).astype(BF16)


def grad_body(norm_ref, z_ref, dy_ref, dz_ref, grad_ref, outs, cfg):
    _, _, width, _, rank = cfg
    target = grad_ref if len(outs) > 1 else outs[0]
    step = step_of(width)
    for c in range(0, width, step):
        target[c : c + step, :rank] = dot(norm_ref[:, c : c + step], dz_ref[...], TN).astype(BF16)
        target[c : c + step, rank:] = dot(dy_ref[:, c : c + step], z_ref[...], TN).astype(BF16)
    if len(outs) > 1:
        rows = width // len(outs)
        for k, out in enumerate(outs):
            begin = pl.multiple_of((dp_index() ^ k) * rows, rows)
            out[...] = grad_ref[pl.ds(begin, rows), :]


def loss_body(y_ref, head_ref, pool_ref, poolt_ref, pair_ref, pairt_ref, lenc_ref, lenr_ref, dy_ref, groups):
    rows = pool_ref.shape[2]
    count = pool_ref.shape[1]
    eye = lax.broadcasted_iota(jnp.int32, (count, count), 0) == lax.broadcasted_iota(
        jnp.int32, (count, count), 1
    )
    for g in range(groups):
        at = pl.ds(g * rows, rows)
        pooled = dot(pool_ref[g], y_ref[at, :])
        column = jnp.sum(pooled / lenc_ref[g] * head_ref[...], axis=-1, keepdims=True)
        line = jnp.sum(jnp.where(eye, column, 0.0), axis=0, keepdims=True)
        up = pair_ref[g] * jax.nn.sigmoid(line - column)
        down = pairt_ref[g] * jax.nn.sigmoid(column - line)
        dscore = jnp.sum(up - down, axis=0, keepdims=True)
        scale = jnp.sum(poolt_ref[g] * (dscore / lenr_ref[g]), axis=-1, keepdims=True)
        dy_ref[at, :] = (scale * head_ref[...]).astype(BF16)


def forward_kernel(tick, cfg, *refs):
    x_ref, gain_ref, prob_ref, wv, wb, y_ref, norm_ref, z_ref, value, attn = refs

    @pl.when(lax.axis_index("section") == tick)
    def _():
        forward_body(x_ref, gain_ref, prob_ref, y_ref, norm_ref, z_ref, wv, wb, value, attn, cfg)


def middle_kernel(tick, pieces, cfg, *refs):
    x_ref, gain_ref, prob_ref, probt_ref, wv, wb = refs[:6]
    loss_refs = refs[6:13]
    dx_ref = refs[13]
    outs = refs[14 : 14 + pieces]
    value, attn, y_ref, norm_ref, z_ref, dy_ref, dz_ref, grad_ref = refs[14 + pieces :]

    @pl.when(lax.axis_index("section") == tick)
    def _():
        forward_body(x_ref, gain_ref, prob_ref, y_ref, norm_ref, z_ref, wv, wb, value, attn, cfg)
        loss_body(y_ref, *loss_refs, dy_ref, cfg[0])
        backward_body(dy_ref, x_ref, gain_ref, probt_ref, dx_ref, dz_ref, wv, wb, value, attn, cfg)
        grad_body(norm_ref, z_ref, dy_ref, dz_ref, grad_ref, outs, cfg)


def backward_kernel(tick, pieces, cfg, *refs):
    dy_ref, x_ref, gain_ref, probt_ref, wv, wb, norm_ref, z_ref = refs[:8]
    dx_ref = refs[8 + pieces]
    outs = refs[9 + pieces : 9 + 2 * pieces]
    value, attn, dz_ref, grad_ref = refs[9 + 2 * pieces :]

    @pl.when(lax.axis_index("section") == tick)
    def _():
        backward_body(dy_ref, x_ref, gain_ref, probt_ref, dx_ref, dz_ref, wv, wb, value, attn, cfg)
        grad_body(norm_ref, z_ref, dy_ref, dz_ref, grad_ref, outs, cfg)


def first_kernel(tick, pieces, cfg, *refs):
    dy_ref, wb, norm_ref, z_ref = refs[:4]
    outs = refs[4 : 4 + pieces]
    dz_ref, grad_ref = refs[4 + pieces :]
    hd, rank = cfg[3], cfg[4]

    @pl.when(lax.axis_index("section") == tick)
    def _():
        dz_ref[...] = dot(dy_ref[...], wb[:, hd + rank :]).astype(BF16)
        grad_body(norm_ref, z_ref, dy_ref, dz_ref, grad_ref, outs, cfg)


def adam_kernel(each, *refs):
    parts = refs[: 2 * each]
    m1_ref, m2_ref, new1_ref, new2_ref, update_ref, grad_ref = refs[2 * each :]
    first = lax.axis_index("section") == 0
    for s, here in enumerate((first, jnp.logical_not(first))):

        @pl.when(here)
        def _(s=s):
            grad = parts[s * each][...].astype(F32)
            for part in parts[s * each + 1 : (s + 1) * each]:
                grad = grad + part[...].astype(F32)
            grad_ref[...] = grad

    rank = m1_ref.shape[2]
    for k in range(m1_ref.shape[1]):
        slab = grad_ref[:, k * rank : (k + 1) * rank]
        new1 = 0.9 * m1_ref[:, k, :] + 0.1 * slab
        new2 = 0.999 * m2_ref[:, k, :] + 0.001 * slab * slab
        new1_ref[:, k, :] = new1
        new2_ref[:, k, :] = new2
        update_ref[:, k, :] = new1 / (1.0 - 0.9**10) / (jnp.sqrt(new2 / (1.0 - 0.999**10)) + 1e-08)


def split(size):
    inner = 2 if size % 2 == 0 else 1
    return size // inner, inner


def by_neighbours(size):
    return split(size)[0] <= 4


def by_pairs(size):
    return size <= 8 and size & (size - 1) == 0


def turns(outer):
    steps = []
    for k in range(1, outer // 2 + 1):
        steps.append((-1, k))
        if 2 * k < outer:
            steps.append((1, k))
    return steps


def spread(chunks, size):
    outer, inner = split(size)
    if not by_neighbours(size):
        return [lax.all_gather(chunk, "dp", axis=0, tiled=True) for chunk in chunks]

    def swapped(array):
        pairs = [(z * inner + y, z * inner + (y + 1) % inner) for z in range(outer) for y in range(inner)]
        return lax.ppermute(array, "dp", pairs)

    wholes = []
    for chunk in chunks:
        held = {0: chunk}
        for side, k in turns(outer):
            pairs = [(z * inner + y, (z - side) % outer * inner + y) for z in range(outer) for y in range(inner)]
            held[side * k] = lax.ppermute(held[side * (k - 1)], "dp", pairs)
        order = [0] + [side * k for side, k in turns(outer)]
        arrays, sources = [], []
        for far in order:
            arrays.append(held[far])
            sources.append((far, 0))
            if inner == 2:
                arrays.append(swapped(held[far]))
                sources.append((far, 1))
        cutoff = len(arrays) - inner if outer > 1 else len(arrays)
        whole = assemble(arrays[:cutoff], tuple(sources[:cutoff]), size)
        if cutoff < len(arrays):
            whole = assemble(arrays[cutoff:], tuple(sources[cutoff:]), size, whole)
        wholes.append(whole)
    return wholes


def exchange(pieces, size, sections, due):
    parts = [pieces[0]]
    for k in range(1, size):
        pairs = [(i * sections + s, (i ^ k) * sections + s) for i in range(size) for s in due]
        parts.append(lax.ppermute(pieces[k], ("dp", "section"), pairs))
    return parts


def shards(
    embedded,
    lengths,
    counts,
    labels,
    value_weight,
    output_projection_weight,
    adapter,
    moment1,
    moment2,
    gain,
    position_bias,
    head,
):
    size = lax.axis_size("dp")
    sections = lax.axis_size("section")
    section = lax.axis_index("section")
    groups, passages, seqlen, width = embedded.shape
    rows = passages * seqlen
    total = groups * rows
    hd = value_weight.shape[2]
    heads = position_bias.shape[1]
    rank = adapter.shape[3]
    cfg = (groups, hd // heads, width, hd, rank)
    own = value_weight.shape[1]

    joined = pl.pallas_call(
        pack_kernel,
        out_shape=jax.ShapeDtypeStruct((own, hd + 2 * rank), BF16),
        in_specs=[VMEM, VMEM],
        out_specs=VMEM,
        compiler_params=limit(4),
        name="pack",
    )(output_projection_weight[0], adapter[0])
    wv, wb = spread([value_weight[0], joined], size)

    square = jax.ShapeDtypeStruct((groups, heads, rows, rows), BF16)
    probs, probst = pl.pallas_call(
        prob_kernel,
        out_shape=(square, square),
        in_specs=[SMEM, VMEM],
        out_specs=(VMEM, VMEM),
        compiler_params=limit(8),
        name="prob",
    )(lengths, position_bias[0])
    shapes = [(passages, rows), (rows, passages), (passages, passages), (passages, passages), (passages, 1), (1, passages)]
    types = [BF16] + [F32] * 5
    loss_in = pl.pallas_call(
        pair_kernel,
        out_shape=tuple(jax.ShapeDtypeStruct((groups,) + a, b) for a, b in zip(shapes, types)),
        in_specs=[SMEM, SMEM, VMEM, VMEM],
        out_specs=(VMEM,) * 6,
        compiler_params=limit(4),
        name="pair",
    )(lengths, counts, labels, lengths)
    loss_in = (head[None, :],) + tuple(loss_in)

    pieces = size if by_pairs(size) else 1
    act = jax.ShapeDtypeStruct((total, width), BF16)
    low_act = jax.ShapeDtypeStruct((total, rank), BF16)
    grads = (jax.ShapeDtypeStruct((width // pieces, 2 * rank), BF16),) * pieces
    mixed = [pltpu.VMEM((total, hd), BF16)] * 2
    wide = pltpu.VMEM((total, width), BF16)
    thin = pltpu.VMEM((total, rank), BF16)
    gbuf = pltpu.VMEM((width, 2 * rank), BF16)

    x = embedded.reshape(total, width)
    saved = []
    for tick in range(sections - 1):
        y, normed, z = pl.pallas_call(
            functools.partial(forward_kernel, tick, cfg),
            out_shape=(act, act, low_act),
            in_specs=[VMEM] * 5,
            out_specs=(VMEM,) * 3,
            scratch_shapes=mixed,
            compiler_params=limit(12),
        )(x, gain, probs, wv, wb)
        saved.append((x, normed, z))
        x = lax.ppermute(y, "section", [(tick, tick + 1)])
    last = sections - 1
    dx, *grad = pl.pallas_call(
        functools.partial(middle_kernel, last, pieces, cfg),
        out_shape=(act,) + grads,
        in_specs=[VMEM] * 13,
        out_specs=(VMEM,) * (1 + pieces),
        scratch_shapes=mixed + [wide, wide, thin, wide, thin, gbuf],
        compiler_params=limit(14),
        name="middle",
    )(x, gain, probs, probst, wv, wb, *loss_in)
    later = grad
    for tick in range(last - 1, 0, -1):
        dy = lax.ppermute(dx, "section", [(tick + 1, tick)])
        x, normed, z = saved[tick]
        dx, *grad = pl.pallas_call(
            functools.partial(backward_kernel, tick, pieces, cfg),
            out_shape=(act,) + grads,
            in_specs=[VMEM] * (8 + pieces),
            input_output_aliases={8 + i: 1 + i for i in range(pieces)},
            out_specs=(VMEM,) * (1 + pieces),
            scratch_shapes=mixed + [thin, gbuf],
            compiler_params=limit(13),
        )(dy, x, gain, probst, wv, wb, normed, z, *later)
        later = grad
    if last > 0:
        dy = lax.ppermute(dx, "section", [(1, 0)])
        _, normed, z = saved[0]
        early = pl.pallas_call(
            functools.partial(first_kernel, 0, pieces, cfg),
            out_shape=grads,
            in_specs=[VMEM] * 4,
            out_specs=(VMEM,) * pieces,
            scratch_shapes=[thin, gbuf],
            compiler_params=limit(8),
            name="first",
        )(dy, wb, normed, z)
    else:
        early = later
    if by_pairs(size):
        parts = exchange(early, size, sections, (0,))
        parts += exchange(later, size, sections, range(1, sections))
    else:
        held = jnp.where(section == 0, early[0], later[0]).astype(F32)
        parts = [lax.psum_scatter(held, "dp", scatter_dimension=0, tiled=True)] * 2
    state = jax.ShapeDtypeStruct(moment1.shape[1:], F32)
    outs = pl.pallas_call(
        functools.partial(adam_kernel, len(parts) // 2),
        out_shape=(state, state, state),
        in_specs=[VMEM] * (len(parts) + 2),
        out_specs=(VMEM,) * 3,
        scratch_shapes=[pltpu.VMEM((own, 2 * rank), F32)],
        compiler_params=limit(8),
        name="adam",
    )(*parts, moment1[0], moment2[0])
    return tuple(out[None] for out in outs)


def solution(mesh):
    in_specs = (
        P("dp", None, None, None),
        P("dp", None),
        P("dp"),
        P("dp", None),
        P("section", "dp", None),
        P("section", "dp", None),
        P("section", "dp", None, None),
        P("section", "dp", None, None),
        P("section", "dp", None, None),
        P("section", None),
        P("section", None, None, None),
        P(),
    )
    out_specs = (
        P("section", "dp", None, None),
        P("section", "dp", None, None),
        P("section", "dp", None, None),
    )
    return jax.shard_map(shards, mesh=mesh, in_specs=in_specs, out_specs=out_specs, check_vma=False)
```

time: 338 us -> 142 us (0.42)
  waiting for transfers between devices: 210 us -> 59.5 us
  starting transfers between devices: 26.7 us -> 66.6 us
  blocking collectives: 34.2 us -> 0 us
  other arithmetic: 20.7 us -> 0 us
  local copies, waits for them, and re-layouts: 21.8 us -> 5.04 us
  between operations: 15.5 us -> 1.78 us
  Pallas kernels: 0 us -> 8.15 us
  matrix products: 7.78 us -> 0 us
    all_gather x2 -> x0, waiting for transfers between devices: 69.2 us -> none  [the longest x1 50.3 us: shards(): lax.all_gather(shard[1], 'dp', axis=0, tiled=True)]
    reduce_scatter x1 -> x0, waiting for transfers between devices: 66.9 us -> none  [shards(): lax.psum_scatter(total + extra, 'dp', scatter_dimension=0, tiled=True)]
    ppermute x6 -> x34, starting transfers between devices: 26.6 us -> 66.6 us  [the longest x14 31.2 us: exchange(): parts.append(lax.ppermute(pieces[k], ('dp', 'section'), pairs))]
    all_gather x1 -> x0, blocking collectives: 34.2 us -> none  [shards(): lax.all_gather(shard[2], 'dp', axis=0, tiled=True)]
    ppermute x6 -> x34, waiting for transfers between devices: 72 us -> 59.5 us  [the longest x1 22.1 us: shards(): dy = lax.ppermute(dx, 'section', [(1, 0)])]
    select_n x12 -> x0, other arithmetic: 10.4 us -> none  [the longest x5 4.91 us: store(): kept = jnp.where(active, value, pick(buffer, position))]
    another operation x13 -> x0, local copies, waits for them, and re-layouts: 8.56 us -> none
    pallas_call x0 -> x15, Pallas kernels: none -> 8.15 us  [the longest x1 2.44 us: shards(): pl.pallas_call(prob_kernel, out_shape=(square, square), in_specs=[SMEM, V...]
  transfers between devices with their start and end apart: 9 -> 34, of which waited for: 7 -> 11; matrix products, arithmetic and copies ran while one was open for 2% -> 0% of each run, Pallas kernels for 0% -> 3%
where the time goes in v1:
time: 142 us; the launch traced here: 141 us
  starting transfers between devices  66.6 us (47%)
  waiting for transfers between devices  59.5 us (42%)
  Pallas kernels  8.15 us (6%)
  local copies, waits for them, and re-layouts  5.04 us (4%)
  between operations  1.78 us (1%)
    ppermute x14, starting transfers between devices, exchange(): parts.append(lax.ppermute(pieces[k], ('dp', 'section'), pairs))  31.2 us
    ppermute x1, waiting for transfers between devices, shards(): dy = lax.ppermute(dx, 'section', [(1, 0)])  22.1 us
    ppermute x6, starting transfers between devices, spread(): held[side * k] = lax.ppermute(held[side * (k - 1)], 'dp', pairs)  18.7 us
    ppermute x8, waiting for transfers between devices, swapped(): return lax.ppermute(array, 'dp', pairs)  15.5 us
    ppermute x6, waiting for transfers between devices, spread(): held[side * k] = lax.ppermute(held[side * (k - 1)], 'dp', pairs)  15.5 us
    ppermute x8, starting transfers between devices, swapped(): return lax.ppermute(array, 'dp', pairs)  11.1 us
    ppermute x14, waiting for transfers between devices, exchange(): parts.append(lax.ppermute(pieces[k], ('dp', 'section'), pairs))  5.18 us
    unnamed x24, local copies, waits for them, and re-layouts  5.04 us
  transfers between devices with their start and end apart: 34, of which 11 were waited for; matrix products, arithmetic and copies ran while one was open for 0% of the time, Pallas kernels for 3%

profile of v1, /device:TPU:0, one launch (start us, length us, event | category | flops | bytes accessed | tf_op | source)
XLA Modules:
  0.0 141.1 jit_solution(17537660153735015411)
XLA Ops:
  2.6 3.1 %collective-permute-start.7 = (bf16[128,1280]{1,0:T(8,128)(2,1)S(1)}, bf16[128,1280]{1,0:T(8,128)(2,1)S(1)}, u32[]{:S(2)}, u32[]{:S(2)}) collective-permute-start(bf16[128,1280]{1,0:T(8,128)(2,1)S(1)} %pack.1.refs_0_), channel_id=1, source_target_pairs={{0,8},{4,12},{8,16},{12,20},{16,24},{20,28},{24,0},{28,4},{1,9},{5... | collective-permute-start | bytes 983048 | tf_op jit(solution)/shard_map/ppermute | solution.py:354
  5.7 2.1 %collective-permute-start.5 = (bf16[128,1024]{1,0:T(8,128)(2,1)}, bf16[128,1024]{1,0:T(8,128)(2,1)S(1)}, u32[]{:S(2)}, u32[]{:S(2)}) collective-permute-start(bf16[128,1024]{1,0:T(8,128)(2,1)} %bitcast.11), channel_id=1, source_target_pairs={{0,24},{4,28},{8,0},{12,4},{16,8},{20,12},{24,16},{28,20},{1,25},{... | collective-permute-start | bytes 786440 | tf_op jit(solution)/shard_map/ppermute | solution.py:354
  7.8 1.7 %collective-permute-start.3 = (bf16[128,1024]{1,0:T(8,128)(2,1)}, bf16[128,1024]{1,0:T(8,128)(2,1)S(1)}, u32[]{:S(2)}, u32[]{:S(2)}) collective-permute-start(bf16[128,1024]{1,0:T(8,128)(2,1)} %bitcast.13), channel_id=1, source_target_pairs={{0,4},{4,0},{8,12},{12,8},{16,20},{20,16},{24,28},{28,24},{1,5},{5... | collective-permute-start | bytes 786440 | tf_op jit(solution)/shard_map/ppermute | solution.py:347
  9.5 3.8 %collective-permute-start.12 = (bf16[128,1280]{1,0:T(8,128)(2,1)S(1)}, bf16[128,1280]{1,0:T(8,128)(2,1)S(1)}, u32[]{:S(2)}, u32[]{:S(2)}) collective-permute-start(bf16[128,1280]{1,0:T(8,128)(2,1)S(1)} %pack.1.refs_0_), channel_id=1, source_target_pairs={{0,24},{4,28},{8,0},{12,4},{16,8},{20,12},{24,16},{28,20},{1,25},{... | collective-permute-start | bytes 983048 | tf_op jit(solution)/shard_map/ppermute | solution.py:354
  13.3 3.0 %collective-permute-done.7.refs_2_ = bf16[128,1280]{1,0:T(8,128)(2,1)S(1)} collective-permute-done((bf16[128,1280]{1,0:T(8,128)(2,1)S(1)}, bf16[128,1280]{1,0:T(8,128)(2,1)S(1)}, u32[]{:S(2)}, u32[]{:S(2)}) %collective-permute-start.7) | collective-permute-done | bytes 327712 | tf_op jit(solution)/shard_map/ppermute | solution.py:354
  16.4 4.2 %collective-permute-start.8 = (bf16[128,1280]{1,0:T(8,128)(2,1)S(1)}, bf16[128,1280]{1,0:T(8,128)(2,1)S(1)}, u32[]{:S(2)}, u32[]{:S(2)}) collective-permute-start(bf16[128,1280]{1,0:T(8,128)(2,1)S(1)} %collective-permute-done.7.refs_2_), channel_id=1, source_target_pairs={{0,8},{4,12},{8,16},{12,20},{16,24},{20,28},{24,0},{28,4},{1,9},{5... | collective-permute-start | bytes 983048 | tf_op jit(solution)/shard_map/ppermute | solution.py:354
  20.6 1.4 %collective-permute-done.5.refs_4_ = bf16[128,1024]{1,0:T(8,128)(2,1)S(1)} collective-permute-done((bf16[128,1024]{1,0:T(8,128)(2,1)}, bf16[128,1024]{1,0:T(8,128)(2,1)S(1)}, u32[]{:S(2)}, u32[]{:S(2)}) %collective-permute-start.5) | collective-permute-done | bytes 262176 | tf_op jit(solution)/shard_map/ppermute | solution.py:354
  22.1 1.7 %collective-permute-start.6 = (bf16[128,1024]{1,0:T(8,128)(2,1)S(1)}, bf16[128,1024]{1,0:T(8,128)(2,1)S(1)}, u32[]{:S(2)}, u32[]{:S(2)}) collective-permute-start(bf16[128,1024]{1,0:T(8,128)(2,1)S(1)} %collective-permute-done.5.refs_4_), channel_id=1, source_target_pairs={{0,4},{4,0},{8,12},{12,8},{16,20},{20,16},{24,28},{28,24},{1,5},{5... | collective-permute-start | bytes 786440 | tf_op jit(solution)/shard_map/ppermute | solution.py:347
  23.8 3.9 %collective-permute-done.refs_2_ = bf16[128,1024]{1,0:T(8,128)(2,1)S(1)} collective-permute-done((bf16[128,1024]{1,0:T(8,128)(2,1)}, bf16[128,1024]{1,0:T(8,128)(2,1)S(1)}, u32[]{:S(2)}, u32[]{:S(2)}) %collective-permute-start) | collective-permute-done | bytes 262176 | tf_op jit(solution)/shard_map/ppermute | solution.py:354
  27.7 1.7 %collective-permute-start.4 = (bf16[128,1024]{1,0:T(8,128)(2,1)S(1)}, bf16[128,1024]{1,0:T(8,128)(2,1)S(1)}, u32[]{:S(2)}, u32[]{:S(2)}) collective-permute-start(bf16[128,1024]{1,0:T(8,128)(2,1)S(1)} %collective-permute-done.refs_2_), channel_id=1, source_target_pairs={{0,4},{4,0},{8,12},{12,8},{16,20},{20,16},{24,28},{28,24},{1,5},{5... | collective-permute-start | bytes 786440 | tf_op jit(solution)/shard_map/ppermute | solution.py:347
  29.4 5.4 %collective-permute-start.1 = (bf16[128,1024]{1,0:T(8,128)(2,1)S(1)}, bf16[128,1024]{1,0:T(8,128)(2,1)S(1)}, u32[]{:S(2)}, u32[]{:S(2)}) collective-permute-start(bf16[128,1024]{1,0:T(8,128)(2,1)S(1)} %collective-permute-done.refs_2_), channel_id=1, source_target_pairs={{0,8},{4,12},{8,16},{12,20},{16,24},{20,28},{24,0},{28,4},{1,9},{5... | collective-permute-start | bytes 786440 | tf_op jit(solution)/shard_map/ppermute | solution.py:354
  35.5 1.3 collective-permute-start.13
  37.6 4.1 %collective-permute-done.8.refs_0_ = bf16[128,1280]{1,0:T(8,128)(2,1)S(1)} collective-permute-done((bf16[128,1280]{1,0:T(8,128)(2,1)S(1)}, bf16[128,1280]{1,0:T(8,128)(2,1)S(1)}, u32[]{:S(2)}, u32[]{:S(2)}) %collective-permute-start.8) | collective-permute-done | bytes 327712 | tf_op jit(solution)/shard_map/ppermute | solution.py:354
  41.7 1.7 %collective-permute-start.9 = (bf16[128,1280]{1,0:T(8,128)(2,1)S(1)}, bf16[128,1280]{1,0:T(8,128)(2,1)S(1)}, u32[]{:S(2)}, u32[]{:S(2)}) collective-permute-start(bf16[128,1280]{1,0:T(8,128)(2,1)S(1)} %collective-permute-done.8.refs_0_), channel_id=1, source_target_pairs={{0,4},{4,0},{8,12},{12,8},{16,20},{20,16},{24,28},{28,24},{1,5},{5... | collective-permute-start | bytes 983048 | tf_op jit(solution)/shard_map/ppermute | solution.py:347
  43.4 3.0 %collective-permute-done.1.refs_0_ = bf16[128,1024]{1,0:T(8,128)(2,1)S(1)} collective-permute-done((bf16[128,1024]{1,0:T(8,128)(2,1)S(1)}, bf16[128,1024]{1,0:T(8,128)(2,1)S(1)}, u32[]{:S(2)}, u32[]{:S(2)}) %collective-permute-start.1) | collective-permute-done | bytes 262176 | tf_op jit(solution)/shard_map/ppermute | solution.py:354
  46.5 1.5 %collective-permute-start.2 = (bf16[128,1024]{1,0:T(8,128)(2,1)S(1)}, bf16[128,1024]{1,0:T(8,128)(2,1)S(1)}, u32[]{:S(2)}, u32[]{:S(2)}) collective-permute-start(bf16[128,1024]{1,0:T(8,128)(2,1)S(1)} %collective-permute-done.1.refs_0_), channel_id=1, source_target_pairs={{0,4},{4,0},{8,12},{12,8},{16,20},{20,16},{24,28},{28,24},{1,5},{5... | collective-permute-start | bytes 786440 | tf_op jit(solution)/shard_map/ppermute | solution.py:347
  49.5 2.4 %prob.1 = (bf16[1,16,128,128]{3,2,1,0:T(8,128)(2,1)S(1)}, bf16[1,16,128,128]{3,2,1,0:T(8,128)(2,1)S(1)}) custom-call(s32[1,8]{1,0:T(1,128)S(1)} %copy-done.8, f32[16,16,16]{2,1,0:T(8,128)S(1)} %bitcast.19), custom_call_target="tpu_custom_call" | custom-call | tf_op jit(solution)/shard_map/prob/pallas_call | solution.py:416
  53.1 6.3 %collective-permute-done.11.refs_3_ = bf16[128,1280]{1,0:T(8,128)(2,1)S(1)} collective-permute-done((bf16[128,1280]{1,0:T(8,128)(2,1)S(1)}, bf16[128,1280]{1,0:T(8,128)(2,1)S(1)}, u32[]{:S(2)}, u32[]{:S(2)}) %collective-permute-start.11) | collective-permute-done | bytes 327712 | tf_op jit(solution)/shard_map/ppermute | solution.py:347
  60.2 9.2 %collective-permute-done.2.refs_1_ = bf16[128,1024]{1,0:T(8,128)(2,1)S(1)} collective-permute-done((bf16[128,1024]{1,0:T(8,128)(2,1)S(1)}, bf16[128,1024]{1,0:T(8,128)(2,1)S(1)}, u32[]{:S(2)}, u32[]{:S(2)}) %collective-permute-start.2) | collective-permute-done | bytes 262176 | tf_op jit(solution)/shard_map/ppermute | solution.py:347
  70.4 1.6 %shard_map.139 = (bf16[128,1024]{1,0:T(8,128)(2,1)S(1)}, bf16[128,1024]{1,0:T(8,128)(2,1)S(1)}, bf16[128,128]{1,0:T(8,128)(2,1)S(1)}) custom-call(bf16[128,1024]{1,0:T(8,128)(2,1)S(1)} %bitcast.15, f32[1,1024]{1,0:T(1,128)S(1)} %copy-done.3, bf16[1,16,128,128]{3,2,1,0:T(8,128)(2,1)S(1)} %get-tuple-element.58.refs_2_, ...), custom_call_target="tpu_custom_call" | custom-call | tf_op jit(solution)/shard_map/pallas_call | solution.py:448
  72.0 1.3 collective-permute-start.14
  79.1 1.4 %collective-permute-start.19 = (bf16[128,1024]{1,0:T(8,128)(2,1)S(1)}, bf16[128,1024]{1,0:T(8,128)(2,1)S(1)}, u32[]{:S(2)}, u32[]{:S(2)}) collective-permute-start(bf16[128,1024]{1,0:T(8,128)(2,1)S(1)} %get-tuple-element.91), channel_id=1, source_target_pairs={{1,0},{5,4},{9,8},{13,12},{17,16},{21,20},{25,24},{29,28}} | collective-permute-start | bytes 786440 | tf_op jit(solution)/shard_map/ppermute | solution.py:483
  83.2 22.1 %collective-permute-done.19.refs_0_ = bf16[128,1024]{1,0:T(8,128)(2,1)S(1)} collective-permute-done((bf16[128,1024]{1,0:T(8,128)(2,1)S(1)}, bf16[128,1024]{1,0:T(8,128)(2,1)S(1)}, u32[]{:S(2)}, u32[]{:S(2)}) %collective-permute-start.19) | collective-permute-done | bytes 262176 | tf_op jit(solution)/shard_map/ppermute | solution.py:483
  107.9 3.6 %collective-permute-start.20 = (bf16[128,256]{1,0:T(8,128)(2,1)S(1)}, bf16[128,256]{1,0:T(8,128)(2,1)S(1)}, u32[]{:S(2)}, u32[]{:S(2)}) collective-permute-start(bf16[128,256]{1,0:T(8,128)(2,1)S(1)} %get-tuple-element.95), channel_id=1, source_target_pairs={{0,4},{4,0},{8,12},{12,8},{16,20},{20,16},{24,28},{28,24}} | collective-permute-start | bytes 196616 | tf_op jit(solution)/shard_map/ppermute | solution.py:375
  111.5 5.8 %collective-permute-start.21 = (bf16[128,256]{1,0:T(8,128)(2,1)S(1)}, bf16[128,256]{1,0:T(8,128)(2,1)S(1)}, u32[]{:S(2)}, u32[]{:S(2)}) collective-permute-start(bf16[128,256]{1,0:T(8,128)(2,1)S(1)} %get-tuple-element.96), channel_id=1, source_target_pairs={{0,8},{4,12},{8,0},{12,4},{16,24},{20,28},{24,16},{28,20}} | collective-permute-start | bytes 196616 | tf_op jit(solution)/shard_map/ppermute | solution.py:375
  117.3 1.9 %collective-permute-start.22 = (bf16[128,256]{1,0:T(8,128)(2,1)S(1)}, bf16[128,256]{1,0:T(8,128)(2,1)S(1)}, u32[]{:S(2)}, u32[]{:S(2)}) collective-permute-start(bf16[128,256]{1,0:T(8,128)(2,1)S(1)} %get-tuple-element.97), channel_id=1, source_target_pairs={{0,12},{4,8},{8,4},{12,0},{16,28},{20,24},{24,20},{28,16}} | collective-permute-start | bytes 196616 | tf_op jit(solution)/shard_map/ppermute | solution.py:375
  119.3 3.2 %collective-permute-start.23 = (bf16[128,256]{1,0:T(8,128)(2,1)S(1)}, bf16[128,256]{1,0:T(8,128)(2,1)S(1)}, u32[]{:S(2)}, u32[]{:S(2)}) collective-permute-start(bf16[128,256]{1,0:T(8,128)(2,1)S(1)} %get-tuple-element.98), channel_id=1, source_target_pairs={{0,16},{4,20},{8,24},{12,28},{16,0},{20,4},{24,8},{28,12}} | collective-permute-start | bytes 196616 | tf_op jit(solution)/shard_map/ppermute | solution.py:375
  122.5 4.4 %collective-permute-start.24 = (bf16[128,256]{1,0:T(8,128)(2,1)S(1)}, bf16[128,256]{1,0:T(8,128)(2,1)S(1)}, u32[]{:S(2)}, u32[]{:S(2)}) collective-permute-start(bf16[128,256]{1,0:T(8,128)(2,1)S(1)} %get-tuple-element.99), channel_id=1, source_target_pairs={{0,20},{4,16},{8,28},{12,24},{16,4},{20,0},{24,12},{28,8}} | collective-permute-start | bytes 196616 | tf_op jit(solution)/shard_map/ppermute | solution.py:375
  126.9 4.0 %collective-permute-start.25 = (bf16[128,256]{1,0:T(8,128)(2,1)S(1)}, bf16[128,256]{1,0:T(8,128)(2,1)S(1)}, u32[]{:S(2)}, u32[]{:S(2)}) collective-permute-start(bf16[128,256]{1,0:T(8,128)(2,1)S(1)} %get-tuple-element.100), channel_id=1, source_target_pairs={{0,24},{4,28},{8,16},{12,20},{16,8},{20,12},{24,0},{28,4}} | collective-permute-start | bytes 196616 | tf_op jit(solution)/shard_map/ppermute | solution.py:375
  130.9 3.7 %collective-permute-start.26 = (bf16[128,256]{1,0:T(8,128)(2,1)S(1)}, bf16[128,256]{1,0:T(8,128)(2,1)S(1)}, u32[]{:S(2)}, u32[]{:S(2)}) collective-permute-start(bf16[128,256]{1,0:T(8,128)(2,1)S(1)} %get-tuple-element.101), channel_id=1, source_target_pairs={{0,28},{4,24},{8,20},{12,16},{16,12},{20,8},{24,4},{28,0}} | collective-permute-start | bytes 196616 | tf_op jit(solution)/shard_map/ppermute | solution.py:375
  135.0 4.8 %collective-permute-done.26.refs_7_ = bf16[128,256]{1,0:T(8,128)(2,1)S(1)} collective-permute-done((bf16[128,256]{1,0:T(8,128)(2,1)S(1)}, bf16[128,256]{1,0:T(8,128)(2,1)S(1)}, u32[]{:S(2)}, u32[]{:S(2)}) %collective-permute-start.26) | collective-permute-done | bytes 65568 | tf_op jit(solution)/shard_map/ppermute | solution.py:375
  139.8 1.3 adam.1
  (75 shorter events, 18.3 us)
Async XLA Ops:
  2.6 13.7 %collective-permute-start.7 = (bf16[128,1280]{1,0:T(8,128)(2,1)S(1)}, bf16[128,1280]{1,0:T(8,128)(2,1)S(1)}, u32[]{:S(2)}, u32[]{:S(2)}) collective-permute-start(bf16[128,1280]{1,0:T(8,128)(2,1)S(1)} %pack.1.refs_0_), channel_id=1, source_target_pairs={{0,8},{4,12},{8,16},{12,20},{16,24},{20,28},{24,0},{28,4},{1,9},{5... | collective-permute-start | bytes 983048 | tf_op jit(solution)/shard_map/ppermute | solution.py:354
  5.7 16.3 %collective-permute-start.5 = (bf16[128,1024]{1,0:T(8,128)(2,1)}, bf16[128,1024]{1,0:T(8,128)(2,1)S(1)}, u32[]{:S(2)}, u32[]{:S(2)}) collective-permute-start(bf16[128,1024]{1,0:T(8,128)(2,1)} %bitcast.11), channel_id=1, source_target_pairs={{0,24},{4,28},{8,0},{12,4},{16,8},{20,12},{24,16},{28,20},{1,25},{... | collective-permute-start | bytes 786440 | tf_op jit(solution)/shard_map/ppermute | solution.py:354
  7.8 19.8 %collective-permute-start = (bf16[128,1024]{1,0:T(8,128)(2,1)}, bf16[128,1024]{1,0:T(8,128)(2,1)S(1)}, u32[]{:S(2)}, u32[]{:S(2)}) collective-permute-start(bf16[128,1024]{1,0:T(8,128)(2,1)} %bitcast.12), channel_id=1, source_target_pairs={{0,8},{4,12},{8,16},{12,20},{16,24},{20,28},{24,0},{28,4},{1,9},{5... | collective-permute-start | bytes 786440 | tf_op jit(solution)/shard_map/ppermute | solution.py:354
  7.8 21.6 %collective-permute-start.3 = (bf16[128,1024]{1,0:T(8,128)(2,1)}, bf16[128,1024]{1,0:T(8,128)(2,1)S(1)}, u32[]{:S(2)}, u32[]{:S(2)}) collective-permute-start(bf16[128,1024]{1,0:T(8,128)(2,1)} %bitcast.13), channel_id=1, source_target_pairs={{0,4},{4,0},{8,12},{12,8},{16,20},{20,16},{24,28},{28,24},{1,5},{5... | collective-permute-start | bytes 786440 | tf_op jit(solution)/shard_map/ppermute | solution.py:347
  9.5 25.3 %collective-permute-start.12 = (bf16[128,1280]{1,0:T(8,128)(2,1)S(1)}, bf16[128,1280]{1,0:T(8,128)(2,1)S(1)}, u32[]{:S(2)}, u32[]{:S(2)}) collective-permute-start(bf16[128,1280]{1,0:T(8,128)(2,1)S(1)} %pack.1.refs_0_), channel_id=1, source_target_pairs={{0,24},{4,28},{8,0},{12,4},{16,8},{20,12},{24,16},{28,20},{1,25},{... | collective-permute-start | bytes 983048 | tf_op jit(solution)/shard_map/ppermute | solution.py:354
  16.4 25.3 %collective-permute-start.8 = (bf16[128,1280]{1,0:T(8,128)(2,1)S(1)}, bf16[128,1280]{1,0:T(8,128)(2,1)S(1)}, u32[]{:S(2)}, u32[]{:S(2)}) collective-permute-start(bf16[128,1280]{1,0:T(8,128)(2,1)S(1)} %collective-permute-done.7.refs_2_), channel_id=1, source_target_pairs={{0,8},{4,12},{8,16},{12,20},{16,24},{20,28},{24,0},{28,4},{1,9},{5... | collective-permute-start | bytes 983048 | tf_op jit(solution)/shard_map/ppermute | solution.py:354
  22.1 13.5 %collective-permute-start.6 = (bf16[128,1024]{1,0:T(8,128)(2,1)S(1)}, bf16[128,1024]{1,0:T(8,128)(2,1)S(1)}, u32[]{:S(2)}, u32[]{:S(2)}) collective-permute-start(bf16[128,1024]{1,0:T(8,128)(2,1)S(1)} %collective-permute-done.5.refs_4_), channel_id=1, source_target_pairs={{0,4},{4,0},{8,12},{12,8},{16,20},{20,16},{24,28},{28,24},{1,5},{5... | collective-permute-start | bytes 786440 | tf_op jit(solution)/shard_map/ppermute | solution.py:347
  27.7 9.2 %collective-permute-start.4 = (bf16[128,1024]{1,0:T(8,128)(2,1)S(1)}, bf16[128,1024]{1,0:T(8,128)(2,1)S(1)}, u32[]{:S(2)}, u32[]{:S(2)}) collective-permute-start(bf16[128,1024]{1,0:T(8,128)(2,1)S(1)} %collective-permute-done.refs_2_), channel_id=1, source_target_pairs={{0,4},{4,0},{8,12},{12,8},{16,20},{20,16},{24,28},{28,24},{1,5},{5... | collective-permute-start | bytes 786440 | tf_op jit(solution)/shard_map/ppermute | solution.py:347
  29.4 17.1 %collective-permute-start.1 = (bf16[128,1024]{1,0:T(8,128)(2,1)S(1)}, bf16[128,1024]{1,0:T(8,128)(2,1)S(1)}, u32[]{:S(2)}, u32[]{:S(2)}) collective-permute-start(bf16[128,1024]{1,0:T(8,128)(2,1)S(1)} %collective-permute-done.refs_2_), channel_id=1, source_target_pairs={{0,8},{4,12},{8,16},{12,20},{16,24},{20,28},{24,0},{28,4},{1,9},{5... | collective-permute-start | bytes 786440 | tf_op jit(solution)/shard_map/ppermute | solution.py:354
  34.8 18.3 %collective-permute-start.10 = (bf16[128,1280]{1,0:T(8,128)(2,1)S(1)}, bf16[128,1280]{1,0:T(8,128)(2,1)S(1)}, u32[]{:S(2)}, u32[]{:S(2)}) collective-permute-start(bf16[128,1280]{1,0:T(8,128)(2,1)S(1)} %pack.1.refs_0_), channel_id=1, source_target_pairs={{0,4},{4,0},{8,12},{12,8},{16,20},{20,16},{24,28},{28,24},{1,5},{5... | collective-permute-start | bytes 983048 | tf_op jit(solution)/shard_map/ppermute | solution.py:347
  35.5 17.6 %collective-permute-start.13 = (bf16[128,1280]{1,0:T(8,128)(2,1)S(1)}, bf16[128,1280]{1,0:T(8,128)(2,1)S(1)}, u32[]{:S(2)}, u32[]{:S(2)}) collective-permute-start(bf16[128,1280]{1,0:T(8,128)(2,1)S(1)} %collective-permute-done.12.refs_4_), channel_id=1, source_target_pairs={{0,4},{4,0},{8,12},{12,8},{16,20},{20,16},{24,28},{28,24},{1,5},{5... | collective-permute-start | bytes 983048 | tf_op jit(solution)/shard_map/ppermute | solution.py:347
  36.9 22.6 %collective-permute-start.11 = (bf16[128,1280]{1,0:T(8,128)(2,1)S(1)}, bf16[128,1280]{1,0:T(8,128)(2,1)S(1)}, u32[]{:S(2)}, u32[]{:S(2)}) collective-permute-start(bf16[128,1280]{1,0:T(8,128)(2,1)S(1)} %collective-permute-done.7.refs_2_), channel_id=1, source_target_pairs={{0,4},{4,0},{8,12},{12,8},{16,20},{20,16},{24,28},{28,24},{1,5},{5... | collective-permute-start | bytes 983048 | tf_op jit(solution)/shard_map/ppermute | solution.py:347
  41.7 27.7 %collective-permute-start.9 = (bf16[128,1280]{1,0:T(8,128)(2,1)S(1)}, bf16[128,1280]{1,0:T(8,128)(2,1)S(1)}, u32[]{:S(2)}, u32[]{:S(2)}) collective-permute-start(bf16[128,1280]{1,0:T(8,128)(2,1)S(1)} %collective-permute-done.8.refs_0_), channel_id=1, source_target_pairs={{0,4},{4,0},{8,12},{12,8},{16,20},{20,16},{24,28},{28,24},{1,5},{5... | collective-permute-start | bytes 983048 | tf_op jit(solution)/shard_map/ppermute | solution.py:347
  46.5 22.9 %collective-permute-start.2 = (bf16[128,1024]{1,0:T(8,128)(2,1)S(1)}, bf16[128,1024]{1,0:T(8,128)(2,1)S(1)}, u32[]{:S(2)}, u32[]{:S(2)}) collective-permute-start(bf16[128,1024]{1,0:T(8,128)(2,1)S(1)} %collective-permute-done.1.refs_0_), channel_id=1, source_target_pairs={{0,4},{4,0},{8,12},{12,8},{16,20},{20,16},{24,28},{28,24},{1,5},{5... | collective-permute-start | bytes 786440 | tf_op jit(solution)/shard_map/ppermute | solution.py:347
  72.0 2.4 %collective-permute-start.14 = (bf16[128,1024]{1,0:T(8,128)(2,1)S(1)}, bf16[128,1024]{1,0:T(8,128)(2,1)S(1)}, u32[]{:S(2)}, u32[]{:S(2)}) collective-permute-start(bf16[128,1024]{1,0:T(8,128)(2,1)S(1)} %get-tuple-element.59), channel_id=1, source_target_pairs={{0,1},{4,5},{8,9},{12,13},{16,17},{20,21},{24,25},{28,29}} | collective-permute-start | bytes 786440 | tf_op jit(solution)/shard_map/ppermute | solution.py:457
  74.4 0.8 collective-permute-start.15
  75.3 2.1 %collective-permute-start.16 = (bf16[128,1024]{1,0:T(8,128)(2,1)S(1)}, bf16[128,1024]{1,0:T(8,128)(2,1)S(1)}, u32[]{:S(2)}, u32[]{:S(2)}) collective-permute-start(bf16[128,1024]{1,0:T(8,128)(2,1)S(1)} %get-tuple-element.61), channel_id=1, source_target_pairs={{2,3},{6,7},{10,11},{14,15},{18,19},{22,23},{26,27},{30,31}} | collective-permute-start | bytes 786440 | tf_op jit(solution)/shard_map/ppermute | solution.py:457
  79.1 26.3 %collective-permute-start.19 = (bf16[128,1024]{1,0:T(8,128)(2,1)S(1)}, bf16[128,1024]{1,0:T(8,128)(2,1)S(1)}, u32[]{:S(2)}, u32[]{:S(2)}) collective-permute-start(bf16[128,1024]{1,0:T(8,128)(2,1)S(1)} %get-tuple-element.91), channel_id=1, source_target_pairs={{1,0},{5,4},{9,8},{13,12},{17,16},{21,20},{25,24},{29,28}} | collective-permute-start | bytes 786440 | tf_op jit(solution)/shard_map/ppermute | solution.py:483
  80.5 26.1 %collective-permute-start.27 = (bf16[128,256]{1,0:T(8,128)(2,1)S(1)}, bf16[128,256]{1,0:T(8,128)(2,1)S(1)}, u32[]{:S(2)}, u32[]{:S(2)}) collective-permute-start(bf16[128,256]{1,0:T(8,128)(2,1)S(1)} %get-tuple-element.103), channel_id=1, source_target_pairs={{1,5},{2,6},{3,7},{5,1},{6,2},{7,3},{9,13},{10,14},{11,15},{13,9},... | collective-permute-start | bytes 196616 | tf_op jit(solution)/shard_map/ppermute | solution.py:375
  81.2 26.1 %collective-permute-start.28 = (bf16[128,256]{1,0:T(8,128)(2,1)S(1)}, bf16[128,256]{1,0:T(8,128)(2,1)S(1)}, u32[]{:S(2)}, u32[]{:S(2)}) collective-permute-start(bf16[128,256]{1,0:T(8,128)(2,1)S(1)} %get-tuple-element.104), channel_id=1, source_target_pairs={{1,9},{2,10},{3,11},{5,13},{6,14},{7,15},{9,1},{10,2},{11,3},{13,5... | collective-permute-start | bytes 196616 | tf_op jit(solution)/shard_map/ppermute | solution.py:375
  81.8 26.1 %collective-permute-start.29 = (bf16[128,256]{1,0:T(8,128)(2,1)S(1)}, bf16[128,256]{1,0:T(8,128)(2,1)S(1)}, u32[]{:S(2)}, u32[]{:S(2)}) collective-permute-start(bf16[128,256]{1,0:T(8,128)(2,1)S(1)} %get-tuple-element.105), channel_id=1, source_target_pairs={{1,13},{2,14},{3,15},{5,9},{6,10},{7,11},{9,5},{10,6},{11,7},{13,1... | collective-permute-start | bytes 196616 | tf_op jit(solution)/shard_map/ppermute | solution.py:375
  82.5 29.0 %collective-permute-start.30 = (bf16[128,256]{1,0:T(8,128)(2,1)S(1)}, bf16[128,256]{1,0:T(8,128)(2,1)S(1)}, u32[]{:S(2)}, u32[]{:S(2)}) collective-permute-start(bf16[128,256]{1,0:T(8,128)(2,1)S(1)} %get-tuple-element.106), channel_id=1, source_target_pairs={{1,17},{2,18},{3,19},{5,21},{6,22},{7,23},{9,25},{10,26},{11,27},{... | collective-permute-start | bytes 196616 | tf_op jit(solution)/shard_map/ppermute | solution.py:375
  105.3 12.0 %collective-permute-start.31 = (bf16[128,256]{1,0:T(8,128)(2,1)S(1)}, bf16[128,256]{1,0:T(8,128)(2,1)S(1)}, u32[]{:S(2)}, u32[]{:S(2)}) collective-permute-start(bf16[128,256]{1,0:T(8,128)(2,1)S(1)} %get-tuple-element.107), channel_id=1, source_target_pairs={{1,21},{2,22},{3,23},{5,17},{6,18},{7,19},{9,29},{10,30},{11,31},{... | collective-permute-start | bytes 196616 | tf_op jit(solution)/shard_map/ppermute | solution.py:375
  106.6 12.7 %collective-permute-start.32 = (bf16[128,256]{1,0:T(8,128)(2,1)S(1)}, bf16[128,256]{1,0:T(8,128)(2,1)S(1)}, u32[]{:S(2)}, u32[]{:S(2)}) collective-permute-start(bf16[128,256]{1,0:T(8,128)(2,1)S(1)} %get-tuple-element.108), channel_id=1, source_target_pairs={{1,25},{2,26},{3,27},{5,29},{6,30},{7,31},{9,17},{10,18},{11,19},{... | collective-permute-start | bytes 196616 | tf_op jit(solution)/shard_map/ppermute | solution.py:375
  107.2 15.3 %collective-permute-start.33 = (bf16[128,256]{1,0:T(8,128)(2,1)S(1)}, bf16[128,256]{1,0:T(8,128)(2,1)S(1)}, u32[]{:S(2)}, u32[]{:S(2)}) collective-permute-start(bf16[128,256]{1,0:T(8,128)(2,1)S(1)} %get-tuple-element.109), channel_id=1, source_target_pairs={{1,29},{2,30},{3,31},{5,25},{6,26},{7,27},{9,21},{10,22},{11,23},{... | collective-permute-start | bytes 196616 | tf_op jit(solution)/shard_map/ppermute | solution.py:375
  107.9 19.0 %collective-permute-start.20 = (bf16[128,256]{1,0:T(8,128)(2,1)S(1)}, bf16[128,256]{1,0:T(8,128)(2,1)S(1)}, u32[]{:S(2)}, u32[]{:S(2)}) collective-permute-start(bf16[128,256]{1,0:T(8,128)(2,1)S(1)} %get-tuple-element.95), channel_id=1, source_target_pairs={{0,4},{4,0},{8,12},{12,8},{16,20},{20,16},{24,28},{28,24}} | collective-permute-start | bytes 196616 | tf_op jit(solution)/shard_map/ppermute | solution.py:375
  111.5 19.4 %collective-permute-start.21 = (bf16[128,256]{1,0:T(8,128)(2,1)S(1)}, bf16[128,256]{1,0:T(8,128)(2,1)S(1)}, u32[]{:S(2)}, u32[]{:S(2)}) collective-permute-start(bf16[128,256]{1,0:T(8,128)(2,1)S(1)} %get-tuple-element.96), channel_id=1, source_target_pairs={{0,8},{4,12},{8,0},{12,4},{16,24},{20,28},{24,16},{28,20}} | collective-permute-start | bytes 196616 | tf_op jit(solution)/shard_map/ppermute | solution.py:375
  117.3 17.3 %collective-permute-start.22 = (bf16[128,256]{1,0:T(8,128)(2,1)S(1)}, bf16[128,256]{1,0:T(8,128)(2,1)S(1)}, u32[]{:S(2)}, u32[]{:S(2)}) collective-permute-start(bf16[128,256]{1,0:T(8,128)(2,1)S(1)} %get-tuple-element.97), channel_id=1, source_target_pairs={{0,12},{4,8},{8,4},{12,0},{16,28},{20,24},{24,20},{28,16}} | collective-permute-start | bytes 196616 | tf_op jit(solution)/shard_map/ppermute | solution.py:375
  119.3 15.4 %collective-permute-start.23 = (bf16[128,256]{1,0:T(8,128)(2,1)S(1)}, bf16[128,256]{1,0:T(8,128)(2,1)S(1)}, u32[]{:S(2)}, u32[]{:S(2)}) collective-permute-start(bf16[128,256]{1,0:T(8,128)(2,1)S(1)} %get-tuple-element.98), channel_id=1, source_target_pairs={{0,16},{4,20},{8,24},{12,28},{16,0},{20,4},{24,8},{28,12}} | collective-permute-start | bytes 196616 | tf_op jit(solution)/shard_map/ppermute | solution.py:375
  122.5 12.1 %collective-permute-start.24 = (bf16[128,256]{1,0:T(8,128)(2,1)S(1)}, bf16[128,256]{1,0:T(8,128)(2,1)S(1)}, u32[]{:S(2)}, u32[]{:S(2)}) collective-permute-start(bf16[128,256]{1,0:T(8,128)(2,1)S(1)} %get-tuple-element.99), channel_id=1, source_target_pairs={{0,20},{4,16},{8,28},{12,24},{16,4},{20,0},{24,12},{28,8}} | collective-permute-start | bytes 196616 | tf_op jit(solution)/shard_map/ppermute | solution.py:375
  126.9 8.1 %collective-permute-start.25 = (bf16[128,256]{1,0:T(8,128)(2,1)S(1)}, bf16[128,256]{1,0:T(8,128)(2,1)S(1)}, u32[]{:S(2)}, u32[]{:S(2)}) collective-permute-start(bf16[128,256]{1,0:T(8,128)(2,1)S(1)} %get-tuple-element.100), channel_id=1, source_target_pairs={{0,24},{4,28},{8,16},{12,20},{16,8},{20,12},{24,0},{28,4}} | collective-permute-start | bytes 196616 | tf_op jit(solution)/shard_map/ppermute | solution.py:375
  130.9 8.9 %collective-permute-start.26 = (bf16[128,256]{1,0:T(8,128)(2,1)S(1)}, bf16[128,256]{1,0:T(8,128)(2,1)S(1)}, u32[]{:S(2)}, u32[]{:S(2)}) collective-permute-start(bf16[128,256]{1,0:T(8,128)(2,1)S(1)} %get-tuple-element.101), channel_id=1, source_target_pairs={{0,28},{4,24},{8,20},{12,16},{16,12},{20,8},{24,4},{28,0}} | collective-permute-start | bytes 196616 | tf_op jit(solution)/shard_map/ppermute | solution.py:375
  (14 other events, 136.5 us)
